TPU v7x, 32 devices: a whole 2x2x4 slice. The times are simulated.
32 devices in a mesh: gx: 4 (over z), gy: 4 (over x, core), col: 2 (over y).
Axes of the slice: x: 2, y: 2, z: 4, core: 2. Of those that a mesh axis runs over, the one named last changes fastest.
Arguments:
- fields: bfloat16 [2, 128, 128, 32, 128], P('col', 'gx', 'gy'), may hold values from -6 to 6
- spectral: bfloat16 [1, 16, 16, 2, 32, 32, 16], P(None, 'gx', 'gy', None, None, 'col'), may hold values from -0.75 to 0.75
- skip_weight: bfloat16 [1, 32, 32], replicated, may hold values from -1 to 1
- skip_bias: float32 [1, 32], replicated, may hold values from -3 to 3
- norm_gain: float32 [1, 32], replicated, may hold values from 0.5 to 1.5
- norm_shift: float32 [1, 32], replicated, may hold values from -3 to 3
Outputs:
- activations: bfloat16 [2, 128, 128, 32, 128], P('col', 'gx', 'gy')
All inputs are finite; a program needn't handle non-finite values.
Results may differ from a plain program's by a relative error of at most 0.012.
Values may be sent and summed in bfloat16 or wider, within the bound.
A program may use at most 128 MiB of HBM per device.

v0:
```python
import math

import jax
import jax.numpy as jnp
from jax import lax
from jax.sharding import PartitionSpec as P

X = 128
Y = 128
Z = 128
MX = 16
MY = 16
MZ = 16


norm_eps = 1e-05


def signed_freqs(count):
    index = jnp.arange(count, dtype=jnp.int32)
    return jnp.where(index < count // 2, index, index - count)


def angles(positions, frequency, length):
    turn_count = positions[:, None] * frequency[None, :] % length
    return turn_count.astype(jnp.float32) * (2.0 * math.pi / length)


def forward_table(positions, frequency, length, factor):
    phase_angle = angles(positions, frequency, length)
    cosine = jnp.cos(phase_angle) * factor
    sine_part = jnp.sin(phase_angle) * factor
    from_real = jnp.stack([cosine, -sine_part], axis=-1)
    from_imag = jnp.stack([sine_part, cosine], axis=-1)
    return jnp.stack([from_real, from_imag], axis=1)


def inverse_table(frequency, positions, length):
    phase_angle = angles(positions, frequency, length).T
    cosine = jnp.cos(phase_angle)
    sine_part = jnp.sin(phase_angle)
    from_real = jnp.stack([cosine, sine_part], axis=-1)
    from_imag = jnp.stack([-sine_part, cosine], axis=-1)
    return jnp.stack([from_real, from_imag], axis=1)


def depth_tables(length, count):
    frequency = jnp.arange(count, dtype=jnp.int32)
    phase_angle = angles(jnp.arange(length, dtype=jnp.int32), frequency, length)
    forward = jnp.concatenate([jnp.cos(phase_angle), -jnp.sin(phase_angle)], axis=1)
    backward = jnp.concatenate([jnp.cos(phase_angle).T, -jnp.sin(phase_angle).T], axis=0)
    return (forward.astype(jnp.bfloat16), backward.astype(jnp.bfloat16))


def mix_modes(spectrum, weight):

    def contract(left, right):
        return jnp.einsum("abcz,abcdz->abdz", left, right, preferred_element_type=jnp.float32)

    real_in = spectrum[:, :, :, 0]
    imag_in = spectrum[:, :, :, 1]
    real_weight = weight[:, :, 0]
    imag_weight = weight[:, :, 1]
    real_out = contract(real_in, real_weight) - contract(imag_in, imag_weight)
    imag_out = contract(real_in, imag_weight) + contract(imag_in, real_weight)
    return jnp.stack([real_out, imag_out], axis=3)


def finish(spectral_part, skip_part, offset, scaling, shift_term):
    pre_norm = spectral_part + skip_part + offset[:, None]
    centre = jnp.mean(pre_norm, axis=2, keepdims=True)
    spread = jnp.mean(jnp.square(pre_norm - centre), axis=2, keepdims=True)
    normed = (pre_norm - centre) * lax.rsqrt(spread + norm_eps) * scaling[:, None] + shift_term[
        :, None
    ]
    return jax.nn.gelu(normed, approximate=False).astype(jnp.bfloat16)


def local(fields, spectral, skip_weight, skip_bias, norm_gain, norm_shift):
    highest = lax.Precision.HIGHEST
    hidden = fields[0]
    tile_first, tile_second, channels, depth_cells = hidden.shape
    first_cells = lax.axis_index("gx") * tile_first + jnp.arange(tile_first, dtype=jnp.int32)
    second_cells = lax.axis_index("gy") * tile_second + jnp.arange(tile_second, dtype=jnp.int32)
    depth_forward, depth_backward = depth_tables(Z, MZ)
    second_forward = forward_table(second_cells, signed_freqs(MY), Y, 1.0).astype(jnp.bfloat16)
    first_forward = forward_table(first_cells, signed_freqs(MX), X, 1.0 / math.sqrt(X * Y * Z))
    first_inverse = inverse_table(signed_freqs(MX), first_cells, X).astype(jnp.bfloat16)
    second_inverse = inverse_table(signed_freqs(MY), second_cells, Y)
    inverse_scale = 1.0 / math.sqrt(MX * MY * MZ)
    amplitude = jnp.dot(
        hidden.reshape(-1, depth_cells), depth_forward, preferred_element_type=jnp.float32
    )
    amplitude = amplitude.astype(jnp.bfloat16).reshape(tile_first, tile_second, channels, 2, MZ)
    along_second = jnp.einsum(
        "xycrz,yrks->xkcsz", amplitude, second_forward, preferred_element_type=jnp.float32
    )
    summed_second = lax.psum_scatter(
        along_second.astype(jnp.bfloat16), "gy", scatter_dimension=1, tiled=True
    ).astype(jnp.float32)
    partial_modes = jnp.einsum("xkcsz,xsjt->jkctz", summed_second, first_forward, precision=highest)
    summed = lax.psum_scatter(
        partial_modes.astype(jnp.bfloat16), "gx", scatter_dimension=0, tiled=True
    )
    weights_here = spectral[0]
    mixed_modes = mix_modes(summed, lax.all_gather(weights_here, "col", axis=4, tiled=True)).astype(
        jnp.bfloat16
    )
    gathered_second = lax.all_gather(mixed_modes, "gy", axis=1, tiled=True)
    full_modes = lax.all_gather(gathered_second, "gx", axis=0, tiled=True)
    rows_first = jnp.einsum(
        "jkcsz,jsxt->xkctz", full_modes, first_inverse, preferred_element_type=jnp.float32
    )
    rows_both = jnp.einsum(
        "xkcsz,ksyt->xyctz", rows_first, second_inverse, precision=highest
    ).astype(jnp.bfloat16)
    spectral_part = jnp.dot(
        rows_both.reshape(-1, 2 * MZ), depth_backward, preferred_element_type=jnp.float32
    )
    spectral_part = (
        spectral_part.reshape(tile_first, tile_second, channels, depth_cells) * inverse_scale
    )
    skip_part = jnp.einsum(
        "oc,xycz->xyoz", skip_weight[0], hidden, preferred_element_type=jnp.float32
    )
    hidden = finish(spectral_part, skip_part, skip_bias[0], norm_gain[0], norm_shift[0])
    return hidden[None]


def solution(mesh):
    placed = (
        P("col", "gx", "gy", None, None),
        P(None, "gx", "gy", None, None, "col", None),
        P(),
        P(),
        P(),
        P(),
    )
    return jax.shard_map(
        local,
        mesh=mesh,
        in_specs=placed,
        out_specs=P("col", "gx", "gy", None, None),
        check_vma=False,
    )
```

profile of v0, /device:TPU:31, one launch (start us, length us, event | category | flops | bytes accessed | tf_op | source)
XLA Modules:
  0.0 265.1 jit_solution(5952482807343169716)
XLA Ops:
  7.4 0.0 copy-start
  7.4 0.0 reduce-scatter.3.cloned.1.call-start
  7.4 0.1 negate_convert_fusion.1
  7.4 6.4 %fusion = bf16[32768,32]{0,1:T(8,128)(2,1)S(1)} fusion(bf16[32768,128]{1,0:T(8,128)(2,1)} %bitcast.159, bf16[128,16]{0,1:T(8,128)(2,1)S(1)} %get-tuple-element.37, bf16[128,16]{0,1:T(8,128)(2,1)S(1)} %get-tuple-element.38), kind=kOutput, calls=%fused_computation.1 | convolution fusion | flops 269500416 | bytes 10493952 | tf_op jit(solution)/shard_map/dot_general | solution.py:91
  13.8 7.9 %reshape.722 = bf16[32,32,32,2,16]{2,1,0,4,3:T(8,128)(2,1)} reshape(bf16[32768,32]{0,1:T(8,128)(2,1)S(1)} %fusion) | data formatting | bytes 4194304 | tf_op jit(solution)/shard_map/reshape | solution.py:94
  21.7 0.2 fusion.88
  21.9 4.7 %fusion.24 = bf16[32,16,32,2,16]{2,1,4,0,3:T(8,128)(2,1)S(1)} fusion(bf16[32,32,32,2,16]{2,1,0,4,3:T(8,128)(2,1)} %reshape.722, bf16[32,1,16,2]{0,2,1,3:T(8,128)(2,1)S(1)} %get-tuple-element.16, bf16[32,1,16,2]{0,2,1,3:T(8,128)(2,1)S(1)} %get-tuple-element.15), kind=kOutput, calls=%fused_computation.37 | convolution fusion | flops 67641344 | bytes 3149824 | tf_op jit(solution)/shard_map/xycrz,yrks->xkcsz/dot_general | solution.py:95
  26.6 3.1 %copy.26 = bf16[32,16,32,2,16]{2,4,3,0,1:T(8,128)(2,1)} copy(bf16[32,16,32,2,16]{2,1,4,0,3:T(8,128)(2,1)S(1)} %fusion.24) | data formatting | bytes 2097152 | tf_op jit(solution)/shard_map/convert_element_type | solution.py:99
  29.7 0.0 reduce-scatter.3.cloned.1.call-update
  29.7 0.0 all-gather.3.cloned.1.call-start
  29.8 0.5 all-gather.3.cloned.1.call-update
  30.3 0.2 reduce-scatter.5.cloned.1.call-start
  30.5 0.1 negate_convert_fusion
  30.6 0.2 fusion.85
  30.8 0.0 copy-done
  30.8 14.8 %fusion.13 = f32[32,32,128,32]{2,3,1,0:T(8,128)} fusion(bf16[1,32,32,32,128]{4,3,2,1,0:T(8,128)(2,1)} %param.6, bf16[1,32,32]{2,1,0:T(8,128)(2,1)S(1)} %copy-done), kind=kOutput, calls=%fused_computation.27 | convolution fusion | flops 268435456 | bytes 25167872 | tf_op jit(solution)/shard_map/oc,xycz->xyoz/dot_general | solution.py:123
  45.6 28.7 %reduce-scatter.3.cloned.1.call-done = bf16[32,4,32,2,16]{2,4,3,0,1:T(8,128)(2,1)} async-done(((bf16[32,16,32,2,16]{2,4,3,0,1:T(8,128)(2,1)}), bf16[32,4,32,2,16]{2,4,3,0,1:T(8,128)(2,1)}) %reduce-scatter.3.cloned.1.call-update) | async-done | bytes 262160 | tf_op jit(solution)/shard_map/reduce_scatter | solution.py:98
  74.3 1.9 fusion.30
  76.2 0.9 copy.29
  77.2 0.0 reduce-scatter.5.cloned.1.call-update
  77.2 10.9 %all-gather.3.cloned.1.call-done = bf16[1,4,4,2,32,32,16]{4,6,5,3,2,1,0:T(8,128)(2,1)} async-done(((bf16[1,4,4,2,32,16,16]{4,6,5,3,2,1,0:T(8,128)(2,1)}), bf16[1,4,4,2,32,32,16]{4,6,5,3,2,1,0:T(8,128)(2,1)}) %all-gather.3.cloned.1.call-update) | async-done | bytes 1048592 | tf_op jit(solution)/shard_map/all_gather | solution.py:106
  88.1 4.5 %slice_bitcast_fusion = (bf16[4,4,32,32,16]{2,4,3,1,0:T(8,128)(2,1)}, bf16[4,4,32,32,16]{2,4,3,1,0:T(8,128)(2,1)S(1)}) fusion(bf16[4,4,2,32,32,16]{3,5,4,2,1,0:T(8,128)(2,1)} %bitcast.161), kind=kLoop, calls=%fused_computation.39 | loop fusion | bytes 2097152 | tf_op jit(solution)/shard_map/squeeze | solution.py:63
  92.7 4.5 %copy.44 = bf16[4,4,32,32,16]{3,2,4,1,0:T(8,128)(2,1)} copy(bf16[4,4,32,32,16]{2,4,3,1,0:T(8,128)(2,1)} %get-tuple-element.5) | data formatting | bytes 1048576 | tf_op jit(solution)/shard_map/squeeze | solution.py:63
  97.2 2.9 %copy.41 = bf16[4,4,32,32,16]{3,2,4,1,0:T(8,128)(2,1)} copy(bf16[4,4,32,32,16]{2,4,3,1,0:T(8,128)(2,1)S(1)} %get-tuple-element.6) | data formatting | bytes 1048576 | tf_op jit(solution)/shard_map/squeeze | solution.py:62
  100.1 0.0 reduce-scatter.5.cloned.1.call-done
  100.1 0.9 slice_bitcast_fusion.3
  101.0 2.2 fusion.39
  103.3 2.3 fusion.37
  105.5 2.3 fusion.35
  107.8 2.2 fusion.41
  110.1 7.3 %all_gather.10 = bf16[4,16,32,2,16]{2,4,3,0,1:T(8,128)(2,1)S(1)} all-gather(bf16[4,4,32,2,16]{2,4,3,0,1:T(8,128)(2,1)S(1)} %pad_maximum_fusion), channel_id=1, replica_groups=mesh['gx'=4,'gy'=4,'col'=2] {'gy'}, dimensions={1}, use_global_device_ids=true | all-gather | bytes 163840 | tf_op jit(solution)/shard_map/all_gather | solution.py:109
  117.4 38.5 %all_gather.11 = bf16[16,16,32,2,16]{2,4,3,1,0:T(8,128)(2,1)S(1)} all-gather(bf16[4,16,32,2,16]{2,4,3,1,0:T(8,128)(2,1)S(1)} %copy.30), channel_id=1, replica_groups=mesh['gx'=4,'gy'=4,'col'=2] {'gx'}, dimensions={0}, use_global_device_ids=true | all-gather | bytes 655360 | tf_op jit(solution)/shard_map/all_gather | solution.py:110
  155.9 1.5 convolution_bitcast_fusion
  157.4 0.0 copy-start.4
  157.4 22.8 %fusion.12 = bf16[32,32,32,2,16]{2,1,4,0,3:T(8,128)(2,1)} fusion(f32[32,16,32,2,16]{2,0,4,1,3:T(8,128)S(1)} %convolution_bitcast_fusion, f32[16,1,32,2]{2,0,3,1:T(8,128)S(1)} %get-tuple-element.10, f32[16,1,32,2]{2,0,3,1:T(8,128)S(1)} %get-tuple-element.9), kind=kOutput, calls=%fused_computation.26 | convolution fusion | flops 403703808 | bytes 4202496 | tf_op jit(solution)/shard_map/xkcsz,ksyt->xyctz/dot_general | solution.py:114
  180.2 10.5 %copy.34 = bf16[32,32,32,2,16]{2,4,3,1,0:T(8,128)(2,1)} copy(bf16[32,32,32,2,16]{2,1,4,0,3:T(8,128)(2,1)} %fusion.12) | data formatting | bytes 4194304 | tf_op jit(solution)/shard_map/convert_element_type | solution.py:116
  190.7 0.0 copy-done.4
  190.7 14.5 %fusion.93 = (f32[32,32,128]{2,1,0:T(8,128)S(1)}, f32[32,32,32,128]{3,2,1,0:T(8,128)}) fusion(f32[32]{0:T(128)S(1)} %bitcast.164, f32[32,32,128,32]{2,3,1,0:T(8,128)} %fusion.13, bf16[32,32,32,32]{2,3,1,0:T(8,128)(2,1)} %bitcast.160, bf16[16,128]{1,0:T(8,128)(2,1)S(1)} %get-tuple-element.41, bf16[16,128]{1,0:T(8,128)(2,1)S(1)} %get-tuple-element.42), kind=kOutput, calls=%fused_computation.167 | convolution fusion | flops 285097984 | bytes 36184192 | tf_op jit(solution)/shard_map/dot_general | solution.py:117
  205.2 0.0 copy-start.2
  205.2 0.0 copy-start.3
  205.2 0.0 copy-start.1
  205.2 10.9 %multiply_reduce_fusion = f32[32,32,128]{2,1,0:T(8,128)S(1)} fusion(f32[32,32,32,128]{3,2,1,0:T(8,128)} %get-tuple-element.36, f32[32,32,128]{2,1,0:T(8,128)S(1)} %broadcast_multiply_fusion), kind=kLoop, calls=%fused_computation.23 | loop fusion | flops 12451840 | bytes 17825792 | tf_op jit(solution)/shard_map/reduce_sum | solution.py:72
  216.2 0.1 add_rsqrt_fusion
  216.2 0.0 copy-done.2
  216.3 0.0 copy-done.3
  216.3 41.4 %fusion.21 = bf16[1,32,32,32,128]{4,3,2,1,0:T(8,128)(2,1)} fusion(f32[32]{0:T(128)S(1)} %bitcast.162, f32[32]{0:T(128)S(1)} %bitcast.163, f32[32,32,128]{2,1,0:T(8,128)S(1)} %add_rsqrt_fusion, f32[32,32,32,128]{3,2,1,0:T(8,128)} %get-tuple-element.36, f32[32,32,128]{2,1,0:T(8,128)S(1)} %broadcast_multiply_fusion), kind=kLoop, calls=%fused_computation.36 | loop fusion | flops 289406976 | bytes 26214656 | tf_op jit(solution)/shard_map/broadcast_in_dim | solution.py:127
  257.7 0.0 copy-done.1
  (11 shorter events, 0.2 us)
Async XLA Ops:
  7.4 23.4 %copy-start = (bf16[1,32,32]{2,1,0:T(8,128)(2,1)S(1)}, bf16[1,32,32]{2,1,0:T(8,128)(2,1)}, u32[]{:S(2)}) copy-start(bf16[1,32,32]{2,1,0:T(8,128)(2,1)} %param.8) | copy-start | bytes 6148
  7.4 66.9 %reduce-scatter.3.cloned.1.call-start = ((), (), s32[]{:S(2)}) async-start(), calls=%async_computation.2 | async-start | bytes 5242880 | tf_op jit(solution)/shard_map/reduce_scatter | solution.py:98
  29.7 58.4 %all-gather.3.cloned.1.call-start = ((), (), s32[]{:S(2)}) async-start(), calls=%async_computation.4 | async-start | bytes 6291456 | tf_op jit(solution)/shard_map/all_gather | solution.py:106
  30.3 69.8 %reduce-scatter.5.cloned.1.call-start = ((), (), s32[]{:S(2)}) async-start(), calls=%async_computation.3 | async-start | bytes 655360 | tf_op jit(solution)/shard_map/reduce_scatter | solution.py:102
  157.4 33.3 %copy-start.4 = (f32[1,32]{1,0:T(1,128)S(1)}, f32[1,32]{1,0:T(1,128)}, u32[]{:S(2)}) copy-start(f32[1,32]{1,0:T(1,128)} %param.9) | copy-start | bytes 388
  205.2 11.1 %copy-start.2 = (f32[1,32]{1,0:T(1,128)S(1)}, f32[1,32]{1,0:T(1,128)}, u32[]{:S(2)}) copy-start(f32[1,32]{1,0:T(1,128)} %param.11) | copy-start | bytes 388
  205.2 11.1 %copy-start.3 = (f32[1,32]{1,0:T(1,128)S(1)}, f32[1,32]{1,0:T(1,128)}, u32[]{:S(2)}) copy-start(f32[1,32]{1,0:T(1,128)} %param.10) | copy-start | bytes 388
  205.2 52.5 %copy-start.1 = (bf16[1,32,32]{2,1,0:T(8,128)(2,1)S(1)}, bf16[1,32,32]{2,1,0:T(8,128)(2,1)}, u32[]{:S(2)}) copy-start(bf16[1,32,32]{2,1,0:T(8,128)(2,1)} %param.8) | copy-start | bytes 6148
Sparse Core Ops, SparseCore 0:
  29.9 44.3 reduce-scatter.2
  77.3 18.8 reduce-scatter.4
Sparse Core Ops, SparseCore 1:
  31.8 56.3 all-gather.2
where the time goes:
time: 269 us; the launch traced here: 265 us
  matrix products  75.5 us (28%)
  other arithmetic  53 us (20%)
  blocking collectives  45.7 us (17%)
  waiting for transfers between devices  40.2 us (15%)
  local copies, waits for them, and re-layouts  35.4 us (13%)
  between operations  15 us (6%)
    broadcast_in_dim x1, other arithmetic, local(): return hidden[None]  41.4 us
    all_gather x1, blocking collectives, local(): full_modes = lax.all_gather(gathered_second, 'gx', axis=0, tiled=True)  38.5 us
    reduce_scatter x1, waiting for transfers between devices, local(): lax.psum_scatter(along_second.astype(jnp.bfloat16), 'gy', scatter_dimensi...  28.7 us
    dot_general x1, matrix products, local(): jnp.einsum('xkcsz,ksyt->xyctz', rows_first, second_inverse, precision=hig...  22.8 us
    dot_general x1, matrix products, local(): jnp.einsum('oc,xycz->xyoz', skip_weight[0], hidden, preferred_element_typ...  14.8 us
    dot_general x1, matrix products, local(): jnp.dot(rows_both.reshape(-1, 2 * MZ), depth_backward, preferred_element_...  14.5 us
    all_gather x1, waiting for transfers between devices, local(): lax.all_gather(weights_here, 'col', axis=4, tiled=True)  10.9 us
    reduce_sum x1, other arithmetic, finish(): spread = jnp.mean(jnp.square(pre_norm - centre), axis=2, keepdims=True)  10.9 us
  transfers between devices with their start and end apart: 3, of which 2 were waited for; matrix products, arithmetic and copies ran while one was open for 11% of the time, Pallas kernels for 0%

commit v1 on v0

v1 whole, which is shorter than its diff:
```python
import functools
import math

import jax
import jax.numpy as jnp
import numpy as np
from jax import lax
from jax.experimental import pallas as pl
from jax.experimental.pallas import tpu as pltpu
from jax.sharding import PartitionSpec as P

norm_eps = 1e-05
BF = jnp.bfloat16
F32 = jnp.float32
MESH = pl.DeviceIdType.MESH


def signed(count):
    index = np.arange(count)
    return np.where(index < count // 2, index, index - count)


def cos_sin(positions, frequency, length):
    turns = (positions[:, None] * frequency[None, :]) % length
    phase = turns * (2.0 * math.pi / length)
    return np.cos(phase), np.sin(phase)


def log2(n):
    assert n & (n - 1) == 0
    return n.bit_length() - 1


def div(i, n):
    return lax.shift_right_logical(i, jnp.int32(log2(n)))


def mod(i, n):
    return lax.bitwise_and(i, jnp.int32(n - 1))


def iota(shape, dim):
    return lax.broadcasted_iota(jnp.int32, shape, dim)


def dot(a, b):
    return jnp.dot(a, b, preferred_element_type=F32)


def expand(table, rows, cols, row_of, col_of, row_key, col_key, first_row=0, less=0.0):
    r, c = table.shape
    left = (row_of(iota((rows, r), 0) + first_row) == iota((rows, r), 1)).astype(F32).astype(BF)
    right = (col_of(iota((c, cols), 1)) == iota((c, cols), 0)).astype(F32).astype(BF)
    full = dot(dot(left, table).astype(BF), right)
    keep = row_key(iota((rows, cols), 0) + first_row) == col_key(iota((rows, cols), 1))
    return (full * jnp.where(keep, 1.0 - less, -less)).astype(BF)


def kron_eye(table, n, store, chunk=256):
    rows, cols = table.shape[0] * n, table.shape[1] * n
    chunk = min(chunk, rows)
    for first in range(0, rows, chunk):
        store(
            first,
            expand(
                table, chunk, cols,
                lambda i: div(i, n), lambda j: div(j, n),
                lambda i: mod(i, n), lambda j: mod(j, n), first,
            ),
        )


def front_kernel(
    sizes,
    fields_ref, spectral_ref, depth_ref, tyf_ref, txf_ref, txi_ref, tyi_ref,
    out_ref,
    ky_ref, total_ref, send_ref, recv_ref, spec_ref, mix_ref, modes_ref, gx_ref, hy_ref, w_ref,
    wsem, send1, recv1, send2, recv2, send3, recv3,
):
    n_gx, n_gy, n_col, xl, yl, C, MY, MZ, kxl, kyl, dl, G, steps = sizes
    nxy, N = n_gx * n_gy, n_gx * n_gy * n_col
    L = 2 * kxl * MZ
    step = pl.program_id(0)
    gx, gy, col = lax.axis_index("gx"), lax.axis_index("gy"), lax.axis_index("col")
    place = gx * n_gy + gy
    me = place * n_col + col

    def target(linear):
        return (linear // (n_gy * n_col), (linear // n_col) % n_gy, linear % n_col)

    weights_copy = pltpu.make_async_copy(spectral_ref, w_ref, wsem)

    @pl.when(step == 0)
    def _():
        barrier = pltpu.get_barrier_semaphore()

        def greet(i, carry):
            px, py, pc = target((me + i) % N)
            pl.semaphore_signal(
                barrier, inc=1, device_id={"gx": px, "gy": py, "col": pc}, device_id_type=MESH
            )
            return carry

        lax.fori_loop(1, N, greet, 0)
        weights_copy.start()

        def put(first, value):
            ky_ref[pl.ds(first, value.shape[0]), :] = value

        kron_eye(tyf_ref[gy], C, put)
        total_ref[...] = jnp.zeros_like(total_ref)

    lhs = jnp.concatenate([fields_ref[g] for g in range(G)], axis=-1)
    amplitude = dot(lhs, depth_ref[...]).astype(BF)
    turned = dot(ky_ref[...], amplitude).astype(BF)
    half = MY * C
    acc = None
    for cs in range(2):
        parts = []
        kron_eye(txf_ref[gx, step, cs], MZ, lambda f, v: parts.append(v))
        kx = parts[0] if len(parts) == 1 else jnp.concatenate(parts, axis=0)
        term = dot(turned[cs * half:(cs + 1) * half], kx)
        acc = term if acc is None else acc + term
    total_ref[...] += acc

    @pl.when(step == steps - 1)
    def _():
        rows = kyl * C
        for b in range(n_gx):
            block = total_ref[:, b * L:(b + 1) * L].astype(BF)
            for q in range(n_gy):
                send_ref[b, q] = block[q * rows:(q + 1) * rows]
        pl.semaphore_wait(pltpu.get_barrier_semaphore(), N - 1)

        def scatter(i):
            other = (place + i) % nxy
            return pltpu.make_async_remote_copy(
                src_ref=send_ref.at[other // n_gy, other % n_gy], dst_ref=recv_ref.at[i],
                send_sem=send1.at[i], recv_sem=recv1.at[i],
                device_id={"gx": other // n_gy, "gy": other % n_gy}, device_id_type=MESH,
            )

        def loop(low, high, body):
            def go(i, carry):
                body(i)
                return carry
            lax.fori_loop(low, high, go, 0)

        loop(1, nxy, lambda i: scatter(i).start())

        for cs in range(2):
            def put(first, value, cs=cs):
                gx_ref[cs, pl.ds(first, value.shape[0]), :] = value
            kron_eye(txi_ref[gx, cs], MZ, put)
        chunk = min(256, yl * C)
        for first in range(0, yl * C, chunk):
            hy_ref[pl.ds(first, chunk), :] = expand(
                tyi_ref[gy], chunk, 2 * MY * C,
                lambda i: div(i, C),
                lambda j: div(j, n_col * kyl * dl) * kyl + mod(div(j, dl), kyl),
                lambda i: mod(i, C),
                lambda j: mod(div(j, kyl * dl), n_col) * dl + mod(j, dl),
                first, 1.0 / C,
            )
        weights_copy.wait()

        sum_ = send_ref[gx, gy].astype(F32)
        for i in range(1, nxy):
            scatter(i).wait_recv()
            sum_ = sum_ + recv_ref[i].astype(F32)
        spec_ref[col] = sum_.astype(BF)

        def share(i):
            return pltpu.make_async_remote_copy(
                src_ref=spec_ref.at[col], dst_ref=spec_ref.at[col],
                send_sem=send2.at[i], recv_sem=recv2.at[i],
                device_id={"col": (col + i) % n_col}, device_id_type=MESH,
            )

        for i in range(1, n_col):
            share(i).start()
        packed = []
        for k in range(kyl):
            real = jnp.concatenate([w_ref[j, k, 0].astype(F32) for j in range(kxl)], axis=-1)
            imag = jnp.concatenate([w_ref[j, k, 1].astype(F32) for j in range(kxl)], axis=-1)
            packed.append((
                jnp.concatenate([real, imag], axis=-1), jnp.concatenate([-imag, real], axis=-1)
            ))
        for i in range(1, n_col):
            share(i).wait_recv()
        for s in range(n_col):
            spec = spec_ref[s].astype(F32)
            re, im = spec[:, :L // 2], spec[:, L // 2:]
            re = jnp.concatenate([re, re], axis=-1)
            im = jnp.concatenate([im, im], axis=-1)
            for k in range(kyl):
                wa, wb = packed[k]
                mixed = jnp.sum(
                    re[k * C:(k + 1) * C][:, None, :] * wa + im[k * C:(k + 1) * C][:, None, :] * wb,
                    axis=0,
                )
                mix_ref[s, k * dl:(k + 1) * dl] = mixed.astype(BF)
        modes_ref[gx, gy, col] = mix_ref[col]

        def gather(i):
            px, py, pc = target((me + i) % N)
            return pltpu.make_async_remote_copy(
                src_ref=mix_ref.at[pc], dst_ref=modes_ref.at[gx, gy, col],
                send_sem=send3.at[i], recv_sem=recv3.at[i],
                device_id={"gx": px, "gy": py, "col": pc}, device_id_type=MESH,
            )

        loop(1, N, lambda i: gather(i).start())
        loop(1, nxy, lambda i: scatter(i).wait_send())
        for i in range(1, n_col):
            share(i).wait_send()
        loop(1, N, lambda i: gather(i).wait_recv())
        full = jnp.concatenate(
            [modes_ref[b].reshape(MY * C, L) for b in range(n_gx)], axis=-1
        )
        first_inverse = jnp.concatenate(
            [dot(full, gx_ref[cs]).astype(BF) for cs in range(2)], axis=0
        )
        out_ref[...] = dot(hy_ref[...], first_inverse).astype(BF)
        loop(1, N, lambda i: gather(i).wait_send())


def back_kernel(
    sizes, rows_ref, fields_ref, depth_ref, skip_ref, bias_ref, gain_ref, shift_ref, out_ref, wbd_ref
):
    G, C, MZ, Z, rows, tile = sizes

    @pl.when(pl.program_id(0) == 0)
    def _():
        weight = skip_ref[...].astype(F32)
        weight = (weight - jnp.mean(weight, axis=0, keepdims=True)).astype(BF)
        wbd_ref[...] = expand(
            weight, tile, tile,
            lambda i: mod(i, C), lambda j: mod(j, C), lambda i: div(i, C), lambda j: div(j, C),
        )

    bias = bias_ref[...]
    bias = (bias - jnp.mean(bias, axis=0, keepdims=True))[None]
    gain = gain_ref[...][None]
    shift = shift_ref[...][None]
    for first in range(0, rows, tile):
        for x in range(0, G, 2):
            hidden = jnp.concatenate(
                [fields_ref[x + k, first:first + tile] for k in range(2)], axis=-1
            )
            pre = dot(wbd_ref[...], hidden) + dot(
                rows_ref[first:first + tile, x * 2 * MZ:(x + 2) * 2 * MZ], depth_ref[...]
            )
            pre = pre.reshape(tile // C, C, 2 * Z) + bias
            spread = jnp.mean(pre * pre, axis=1, keepdims=True)
            normed = pre * (lax.rsqrt(spread + norm_eps) * gain) + shift
            value = (0.5 * normed) * (1.0 + lax.erf(normed * (0.5 ** 0.5)))
            value = value.astype(BF).reshape(tile, 2 * Z)
            for k in range(2):
                out_ref[x + k, first:first + tile] = value[:, k * Z:(k + 1) * Z]


def build(mesh):
    n_gx, n_gy, n_col = (mesh.shape[a] for a in ("gx", "gy", "col"))

    def local(fields, spectral, skip_weight, skip_bias, norm_gain, norm_shift):
        hidden = fields[0]
        xl, yl, C, Z = hidden.shape
        weights = spectral[0]
        kxl, kyl, _, _, dl, MZ = weights.shape
        X, Y, MX, MY = xl * n_gx, yl * n_gy, kxl * n_gx, kyl * n_gy
        G = min(8, xl)
        steps = xl // G
        L = 2 * kxl * MZ
        N, nxy = n_gx * n_gy * n_col, n_gx * n_gy

        cz, sz = cos_sin(np.arange(Z), np.arange(MZ), Z)
        forward = np.concatenate([cz, -sz], axis=1)
        depth_forward = np.kron(np.eye(G), forward)
        backward = np.concatenate([cz.T, -sz.T], axis=0) / math.sqrt(MX * MY * MZ)
        depth_backward = np.kron(np.eye(2), backward)
        cy, sy = cos_sin(np.arange(Y), signed(MY), Y)
        tyf = np.stack([cy, sy]).reshape(2, n_gy, yl, MY).transpose(1, 0, 3, 2)
        tyf = tyf.reshape(n_gy, 2 * MY, yl)
        tyi = np.stack([cy, sy]).reshape(2, n_gy, yl, MY).transpose(1, 2, 0, 3)
        tyi = tyi.reshape(n_gy, yl, 2 * MY)
        cx, sx = cos_sin(np.arange(X), signed(MX), X)
        f = np.stack([
            np.stack([np.stack([cx, -sx], 1), np.stack([sx, cx], 1)], 1),
            np.stack([np.stack([-sx, -cx], 1), np.stack([cx, -sx], 1)], 1),
        ]) / math.sqrt(X * Y * Z)
        f = f.reshape(2, n_gx, steps, G, 2, 2, n_gx, kxl).transpose(1, 2, 0, 3, 4, 6, 5, 7)
        txf = f.reshape(n_gx, steps, 2, 2 * G, 2 * MX)
        b = np.stack([
            np.stack([np.stack([cx, sx]), np.stack([-sx, cx])]),
            np.stack([np.stack([-sx, cx]), np.stack([-cx, -sx])]),
        ])
        b = b.reshape(2, 2, 2, n_gx, xl, n_gx, kxl).transpose(3, 0, 5, 1, 6, 4, 2)
        txi = b.reshape(n_gx, 2, 2 * MX, 2 * xl)
        const = lambda a: jnp.asarray(a.astype(np.float32)).astype(BF)

        cells = hidden.reshape(xl, yl * C, Z)
        whole = lambda shape: pl.BlockSpec(shape, lambda i: (0,) * len(shape))
        sizes = (n_gx, n_gy, n_col, xl, yl, C, MY, MZ, kxl, kyl, dl, G, steps)
        tables = [const(t) for t in (depth_forward, tyf, txf, txi, tyi)]
        rows_both = pl.pallas_call(
            functools.partial(front_kernel, sizes),
            grid=(steps,),
            out_shape=jax.ShapeDtypeStruct((yl * C, xl * 2 * MZ), BF),
            in_specs=[
                pl.BlockSpec((G, yl * C, Z), lambda i: (i, 0, 0)),
                pl.BlockSpec(memory_space=pl.ANY),
            ] + [whole(t.shape) for t in tables],
            out_specs=whole((yl * C, xl * 2 * MZ)),
            scratch_shapes=[
                pltpu.VMEM((2 * MY * C, yl * C), BF),
                pltpu.VMEM((MY * C, 2 * MX * MZ), F32),
                pltpu.VMEM((n_gx, n_gy, kyl * C, L), BF),
                pltpu.VMEM((nxy, kyl * C, L), BF),
                pltpu.VMEM((n_col, kyl * C, L), BF),
                pltpu.VMEM((n_col, kyl * dl, L), BF),
                pltpu.VMEM((n_gx, n_gy, n_col, kyl * dl, L), BF),
                pltpu.VMEM((2, 2 * MX * MZ, 2 * xl * MZ), BF),
                pltpu.VMEM((yl * C, 2 * MY * C), BF),
                pltpu.VMEM(weights.shape, BF),
                pltpu.SemaphoreType.DMA,
                pltpu.SemaphoreType.DMA((nxy,)),
                pltpu.SemaphoreType.DMA((nxy,)),
                pltpu.SemaphoreType.DMA((n_col,)),
                pltpu.SemaphoreType.DMA((n_col,)),
                pltpu.SemaphoreType.DMA((N,)),
                pltpu.SemaphoreType.DMA((N,)),
            ],
            compiler_params=pltpu.CompilerParams(
                collective_id=0, has_side_effects=True, vmem_limit_bytes=60 * 2**20,
                dimension_semantics=("arbitrary",),
            ),
            name="front",
        )(cells, weights, *tables)

        G2 = min(4, xl)
        rows = yl * C
        tile = min(256, rows)
        out = pl.pallas_call(
            functools.partial(back_kernel, (G2, C, MZ, Z, rows, tile)),
            grid=(xl // G2,),
            out_shape=jax.ShapeDtypeStruct(cells.shape, BF),
            in_specs=[
                pl.BlockSpec((rows, G2 * 2 * MZ), lambda i: (0, i)),
                pl.BlockSpec((G2, rows, Z), lambda i: (i, 0, 0)),
                whole((4 * MZ, 2 * Z)), whole((C, C)), whole((C, 1)), whole((C, 1)), whole((C, 1)),
            ],
            out_specs=pl.BlockSpec((G2, rows, Z), lambda i: (i, 0, 0)),
            scratch_shapes=[pltpu.VMEM((tile, tile), BF)],
            compiler_params=pltpu.CompilerParams(
                vmem_limit_bytes=40 * 2**20, dimension_semantics=("arbitrary",)
            ),
            name="back",
        )(
            rows_both, cells, const(depth_backward), skip_weight[0],
            skip_bias[0][:, None], norm_gain[0][:, None], norm_shift[0][:, None],
        )
        return out.reshape(1, xl, yl, C, Z)

    return local


def solution(mesh):
    placed = (
        P("col", "gx", "gy", None, None),
        P(None, "gx", "gy", None, None, "col", None),
        P(), P(), P(), P(),
    )
    return jax.shard_map(
        build(mesh), mesh=mesh, in_specs=placed,
        out_specs=P("col", "gx", "gy", None, None), check_vma=False,
    )
```

time: 269 us -> 75.3 us (0.28); the launches traced: 265 us -> 75 us
  matrix products: 75.5 us -> 0 us
  Pallas kernels: 0 us -> 62.1 us
  other arithmetic: 53 us -> 0 us
  blocking collectives: 45.7 us -> 0 us
  waiting for transfers between devices: 40.2 us -> 0 us
  local copies, waits for them, and re-layouts: 35.4 us -> 12.9 us
  between operations: 15 us -> 0.04 us
    dot_general x11 -> x0, matrix products: 75.5 us -> none  [the longest x1 22.8 us: local(): jnp.einsum('xkcsz,ksyt->xyctz', rows_first, second_inverse, precision=hig...]
    pallas_call x0 -> x2, Pallas kernels: none -> 62.1 us  [the longest x1 50.9 us: local(): pl.pallas_call(functools.partial(front_kernel, sizes), grid=(steps,), out...]
    all_gather x2 -> x0, blocking collectives: 45.7 us -> none  [the longest x1 38.5 us: local(): full_modes = lax.all_gather(gathered_second, 'gx', axis=0, tiled=True)]
    broadcast_in_dim x1 -> x0, other arithmetic: 41.4 us -> none  [local(): return hidden[None]]
    reduce_scatter x2 -> x0, waiting for transfers between devices: 28.7 us -> none  [the longest x1 28.7 us: local(): lax.psum_scatter(along_second.astype(jnp.bfloat16), 'gy', scatter_dimensi...]
    convert_element_type x3 -> x0, local copies, waits for them, and re-layouts: 14.6 us -> none  [the longest x1 10.5 us: local(): rows_both = jnp.einsum('xkcsz,ksyt->xyctz', rows_first, second_inverse, p...]
    squeeze x4 -> x0, local copies, waits for them, and re-layouts: 12.9 us -> none  [the longest x2 9.06 us: mix_modes(): imag_weight = weight[:, :, 1]]
    all_gather x1 -> x0, waiting for transfers between devices: 10.9 us -> none  [local(): lax.all_gather(weights_here, 'col', axis=4, tiled=True)]
  transfers between devices with their start and end apart: 3 -> 0, of which waited for: 2 -> 0; matrix products, arithmetic and copies ran while one was open for 11% -> 0% of each run, Pallas kernels for 0% -> 0%
where the time goes in v1:
time: 75.3 us; the launch traced here: 75 us
  Pallas kernels  62.1 us (82%)
  local copies, waits for them, and re-layouts  12.9 us (17%)
    pallas_call x1, Pallas kernels, local(): pl.pallas_call(functools.partial(front_kernel, sizes), grid=(steps,), out...  50.9 us
    pallas_call x1, Pallas kernels, local(): pl.pallas_call(functools.partial(back_kernel, (G2, C, MZ, Z, rows, tile))...  11.2 us
    unnamed x9, local copies, waits for them, and re-layouts  10.7 us

profile of v1, /device:TPU:31, one launch (start us, length us, event | category | flops | bytes accessed | tf_op | source)
XLA Modules:
  0.0 75.0 jit_solution(13996172225692713061)
XLA Ops:
  0.0 0.7 copy.14.bias_ref
  0.7 0.7 copy.15.gain_ref
  1.5 0.7 copy.16.shift_ref
  2.2 5.7 %copy.13 = bf16[1,4,4,2,32,16,16]{6,5,4,3,2,1,0:T(8,128)(2,1)} copy(bf16[1,4,4,2,32,16,16]{4,6,5,3,2,1,0:T(8,128)(2,1)} %param.13) | data formatting | bytes 1048576 | tf_op args[1]
  7.9 0.0 copy-start.2
  7.9 0.0 copy-start.3
  7.9 50.9 %front.1.rows_ref = bf16[1024,1024]{1,0:T(8,128)(2,1)} custom-call(bf16[32,1024,128]{2,1,0:T(8,128)(2,1)} %bitcast.7, bf16[4,4,2,32,16,16]{5,4,3,2,1,0:T(8,128)(2,1)} %bitcast.10, bf16[1024,256]{1,0:T(8,128)(2,1)} %constant.19.depth_ref, bf16[4,32,32]{2,1,0:T(8,128)(2,1)} %constant.20.tyf_ref, bf16[4,4,2,16,32]{4,3,2,1,0:T(8,128)(2,1)} %constant.21.txf_ref, ...), custom_call_target="tpu_custom_call" | custom-call | tf_op jit(solution)/shard_map/front/pallas_call | solution.py:306
  58.8 0.0 copy-done.2
  58.8 0.0 copy-done.3
  58.8 0.0 copy-start
  58.9 3.4 %copy-done = bf16[1,32,32,32,128]{4,3,2,1,0:T(8,128)(2,1)S(1)} copy-done((bf16[1,32,32,32,128]{4,3,2,1,0:T(8,128)(2,1)S(1)}, bf16[1,32,32,32,128]{4,3,2,1,0:T(8,128)(2,1)}, u32[]{:S(2)}) %copy-start) | copy-done | bytes 8388632
  62.2 0.0 copy-start.1
  62.2 1.6 %copy-done.1 = bf16[1024,1024]{1,0:T(8,128)(2,1)S(1)} copy-done((bf16[1024,1024]{1,0:T(8,128)(2,1)S(1)}, bf16[1024,1024]{1,0:T(8,128)(2,1)}, u32[]{:S(2)}) %copy-start.1) | copy-done | bytes 2097176
  63.8 11.2 %back.1 = bf16[32,1024,128]{2,1,0:T(8,128)(2,1)} custom-call(bf16[1024,1024]{1,0:T(8,128)(2,1)S(1)} %copy-done.1, bf16[32,1024,128]{2,1,0:T(8,128)(2,1)S(1)} %bitcast.8, bf16[64,256]{1,0:T(8,128)(2,1)S(1)} %copy-done.2, bf16[32,32]{1,0:T(8,128)(2,1)S(1)} %bitcast.9, f32[32,1]{1,0:T(8,128)S(1)} %copy.14.bias_ref, f32[32,1]{1,0:T(8,128)S(1)} %copy.15.gain_ref, ...), custom_call_target="tpu_custom_call" | custom-call | tf_op jit(solution)/shard_map/back/pallas_call | solution.py:344
Async XLA Ops:
  7.9 50.9 %copy-start.2 = (bf16[64,256]{1,0:T(8,128)(2,1)S(1)}, bf16[64,256]{1,0:T(8,128)(2,1)}, u32[]{:S(2)}) copy-start(bf16[64,256]{1,0:T(8,128)(2,1)} %constant.24.depth_ref) | copy-start | bytes 98308
  7.9 50.9 %copy-start.3 = (bf16[1,32,32]{2,1,0:T(8,128)(2,1)S(1)}, bf16[1,32,32]{2,1,0:T(8,128)(2,1)}, u32[]{:S(2)}) copy-start(bf16[1,32,32]{2,1,0:T(8,128)(2,1)} %param.14) | copy-start | bytes 6148
  58.8 3.4 %copy-start = (bf16[1,32,32,32,128]{4,3,2,1,0:T(8,128)(2,1)S(1)}, bf16[1,32,32,32,128]{4,3,2,1,0:T(8,128)(2,1)}, u32[]{:S(2)}) copy-start(bf16[1,32,32,32,128]{4,3,2,1,0:T(8,128)(2,1)} %param.12) | copy-start | bytes 25165828
  62.2 1.6 %copy-start.1 = (bf16[1024,1024]{1,0:T(8,128)(2,1)S(1)}, bf16[1024,1024]{1,0:T(8,128)(2,1)}, u32[]{:S(2)}) copy-start(bf16[1024,1024]{1,0:T(8,128)(2,1)} %front.1.rows_ref) | copy-start | bytes 6291460

commit v2 on v1

v2 whole, which is shorter than its diff:
```python
import functools
import math

import jax
import jax.numpy as jnp
import numpy as np
from jax import lax
from jax.experimental import pallas as pl
from jax.experimental.pallas import tpu as pltpu
from jax.sharding import PartitionSpec as P

norm_eps = 1e-05
BF = jnp.bfloat16
F32 = jnp.float32
MESH = pl.DeviceIdType.MESH


def signed(count):
    index = np.arange(count)
    return np.where(index < count // 2, index, index - count)


def cos_sin(positions, frequency, length):
    turns = (positions[:, None] * frequency[None, :]) % length
    phase = turns * (2.0 * math.pi / length)
    return np.cos(phase), np.sin(phase)


def log2(n):
    assert n & (n - 1) == 0
    return n.bit_length() - 1


def div(i, n):
    return lax.shift_right_logical(i, jnp.int32(log2(n)))


def mod(i, n):
    return lax.bitwise_and(i, jnp.int32(n - 1))


def iota(shape, dim):
    return lax.broadcasted_iota(jnp.int32, shape, dim)


def dot(a, b):
    return jnp.dot(a, b, preferred_element_type=F32)


def expand(table, rows, cols, row_of, col_of, row_key, col_key, first_row=0):
    r, c = table.shape
    left = (row_of(iota((rows, r), 0) + first_row) == iota((rows, r), 1)).astype(F32).astype(BF)
    right = (col_of(iota((c, cols), 1)) == iota((c, cols), 0)).astype(F32).astype(BF)
    full = dot(dot(left, table).astype(BF), right)
    keep = row_key(iota((rows, cols), 0) + first_row) == col_key(iota((rows, cols), 1))
    return jnp.where(keep, full, 0.0).astype(BF)


def kron_eye(table, n, store, chunk=256):
    rows, cols = table.shape[0] * n, table.shape[1] * n
    chunk = min(chunk, rows)
    for first in range(0, rows, chunk):
        store(
            first,
            expand(
                table, chunk, cols,
                lambda i: div(i, n), lambda j: div(j, n),
                lambda i: mod(i, n), lambda j: mod(j, n), first,
            ),
        )


def front_kernel(
    sizes,
    fields_ref, spectral_ref, depth_ref, tyf_ref, txf_ref, txi_ref, tyi_ref,
    out_ref,
    ky_ref, kx_ref, total_ref, send_ref, recv_ref, spec_ref, mix_ref, modes_ref, gx_ref, hy_ref,
    cm_ref, w_ref, wa_ref, wb_ref,
    wsem, send1, recv1, send2, recv2, send3, recv3,
):
    n_gx, n_gy, n_col, xl, yl, C, MY, MZ, kxl, kyl, dl, G, steps, halves = sizes
    nxy, N = n_gx * n_gy, n_gx * n_gy * n_col
    L = 2 * kxl * MZ
    CH = C // halves
    per = n_col // halves
    half, step = pl.program_id(0), pl.program_id(1)
    gx, gy, col = lax.axis_index("gx"), lax.axis_index("gy"), lax.axis_index("col")
    place = gx * n_gy + gy
    me = place * n_col + col

    def target(linear):
        return (linear // (n_gy * n_col), (linear // n_col) % n_gy, linear % n_col)

    def loop(low, high, body):
        def go(i, carry):
            body(i)
            return carry
        lax.fori_loop(low, high, go, 0)

    weights_copy = pltpu.make_async_copy(spectral_ref, w_ref, wsem)

    @pl.when((half == 0) & (step == 0))
    def _():
        barrier = pltpu.get_barrier_semaphore()

        def greet(i):
            px, py, pc = target((me + i) % N)
            pl.semaphore_signal(
                barrier, inc=1, device_id={"gx": px, "gy": py, "col": pc}, device_id_type=MESH
            )

        loop(1, N, greet)
        weights_copy.start()

        def put(first, value):
            ky_ref[pl.ds(first, value.shape[0]), :] = value

        kron_eye(tyf_ref[gy], CH, put)

    @pl.when(half == 0)
    def _():
        for cs in range(2):
            def put(first, value, cs=cs):
                kx_ref[step, cs, pl.ds(first, value.shape[0]), :] = value
            kron_eye(txf_ref[gx, step, cs], MZ, put)

    lhs = jnp.concatenate(
        [fields_ref[g].reshape(yl * CH, fields_ref.shape[-1]) for g in range(G)], axis=-1
    )
    amplitude = dot(lhs, depth_ref[...]).astype(BF)
    turned = dot(ky_ref[...], amplitude).astype(BF)
    top = MY * CH
    term = dot(turned[:top], kx_ref[step, 0]) + dot(turned[top:], kx_ref[step, 1])

    @pl.when(step == 0)
    def _():
        total_ref[...] = term

    @pl.when(step > 0)
    def _():
        total_ref[...] += term

    def scatter(h, i):
        other = (place + i) % nxy
        return pltpu.make_async_remote_copy(
            src_ref=send_ref.at[h, other // n_gy, other % n_gy], dst_ref=recv_ref.at[h, i],
            send_sem=send1.at[h, i], recv_sem=recv1.at[h, i],
            device_id={"gx": other // n_gy, "gy": other % n_gy}, device_id_type=MESH,
        )

    @pl.when(step == steps - 1)
    def _():
        rows = kyl * CH
        for b in range(n_gx):
            block = total_ref[:, b * L:(b + 1) * L].astype(BF)
            for q in range(n_gy):
                send_ref[half, b, q] = block[q * rows:(q + 1) * rows]

        @pl.when(half == 0)
        def _():
            pl.semaphore_wait(pltpu.get_barrier_semaphore(), N - 1)

        loop(1, nxy, lambda i: scatter(half, i).start())

    @pl.when((half == halves - 1) & (step == steps - 1))
    def _():
        weights_copy.wait()
        eye = (iota((C, C), 0) == iota((C, C), 1)).astype(F32).astype(BF)
        turn = lambda a: lax.dot_general(
            eye, a, (((1,), (1,)), ((), ())), preferred_element_type=F32
        )
        for k in range(kyl):
            for d in range(dl):
                parts = [[w_ref[j, k, r, d] for j in range(kxl)] for r in range(2)]
                wa_ref[k, d] = turn(jnp.concatenate(parts[0] + parts[1], axis=0))
                wb_ref[k, d] = turn(jnp.concatenate(parts[1] + parts[0], axis=0))
        for cs in range(2):
            def put(first, value, cs=cs):
                gx_ref[cs, pl.ds(first, value.shape[0]), :] = value
            kron_eye(txi_ref[gx, cs], MZ, put)
        chunk = min(256, yl * CH)
        for first in range(0, yl * CH, chunk):
            hy_ref[pl.ds(first, chunk), :] = expand(
                tyi_ref[gy], chunk, 2 * MY * CH,
                lambda i: div(i, CH),
                lambda j: div(j, per * kyl * dl) * kyl + mod(div(j, dl), kyl),
                lambda i: mod(i, CH),
                lambda j: mod(div(j, kyl * dl), per) * dl + mod(j, dl),
                first,
            )
        shape = (MY * C, MY * C)
        i, j = iota(shape, 0), iota(shape, 1)
        in_half = mod(i, MY * CH)
        gy_i = div(in_half, per * kyl * dl)
        col_i = div(i, MY * CH) * per + mod(div(in_half, kyl * dl), per)
        source = (gy_i * n_col + col_i) * (kyl * dl) + mod(in_half, kyl * dl)
        same = (gy_i == div(j, n_col * kyl * dl)) & (mod(div(i, dl), kyl) == mod(div(j, dl), kyl))
        cm_ref[...] = (
            (source == j).astype(F32) - jnp.where(same, 1.0 / C, 0.0)
        ).astype(BF)

        def share(h, i):
            return pltpu.make_async_remote_copy(
                src_ref=spec_ref.at[col, h], dst_ref=spec_ref.at[col, h],
                send_sem=send2.at[h, i], recv_sem=recv2.at[h, i],
                device_id={"col": (col + i) % n_col}, device_id_type=MESH,
            )

        for h in range(halves):
            total = send_ref[h, gx, gy].astype(F32)
            for i in range(1, nxy):
                scatter(h, i).wait_recv()
                total = total + recv_ref[h, i].astype(F32)
            spec_ref[col, h] = total.astype(BF)
            for i in range(1, n_col):
                share(h, i).start()
        for h in range(halves):
            for i in range(1, n_col):
                share(h, i).wait_recv()
        for s in range(n_col):
            left, right = [], []
            for h in range(halves):
                spec = spec_ref[s, h].astype(F32)
                re, im = spec[:, :L // 2], spec[:, L // 2:]
                left.append(jnp.concatenate([re, re], axis=-1))
                right.append(jnp.concatenate([-im, im], axis=-1))
            for k in range(kyl):
                mixed = None
                for h in range(halves):
                    rows, chans = slice(k * CH, (k + 1) * CH), slice(h * CH, (h + 1) * CH)
                    term = left[h][rows][None] * wa_ref[k, :, chans]
                    term = term + right[h][rows][None] * wb_ref[k, :, chans]
                    mixed = term if mixed is None else mixed + term
                mix_ref[s, k * dl:(k + 1) * dl] = jnp.sum(mixed, axis=1).astype(BF)
        modes_ref[gx, gy, col] = mix_ref[col]

        def gather(i):
            px, py, pc = target((me + i) % N)
            return pltpu.make_async_remote_copy(
                src_ref=mix_ref.at[pc], dst_ref=modes_ref.at[gx, gy, col],
                send_sem=send3.at[i], recv_sem=recv3.at[i],
                device_id={"gx": px, "gy": py, "col": pc}, device_id_type=MESH,
            )

        loop(1, N, lambda i: gather(i).start())
        for h in range(halves):
            loop(1, nxy, lambda i: scatter(h, i).wait_send())
            for i in range(1, n_col):
                share(h, i).wait_send()
        loop(1, N, lambda i: gather(i).wait_recv())
        full = jnp.concatenate(
            [modes_ref[b].reshape(MY * C, L) for b in range(n_gx)], axis=-1
        )
        full = dot(cm_ref[...], full).astype(BF)
        for h in range(halves):
            part = full[h * MY * CH:(h + 1) * MY * CH]
            part = jnp.concatenate([dot(part, gx_ref[cs]).astype(BF) for cs in range(2)], axis=0)
            out_ref[:, h * CH:(h + 1) * CH] = dot(hy_ref[...], part).astype(BF).reshape(
                yl, CH, out_ref.shape[-1]
            )
        loop(1, N, lambda i: gather(i).wait_send())


def back_kernel(
    sizes, rows_ref, fields_ref, depth_ref, skip_ref, bias_ref, gain_ref, shift_ref, out_ref, wbd_ref
):
    G, C, MZ, Z, rows, tile = sizes

    @pl.when(pl.program_id(0) == 0)
    def _():
        weight = skip_ref[...].astype(F32)
        weight = (weight - jnp.mean(weight, axis=0, keepdims=True)).astype(BF)
        wbd_ref[...] = expand(
            weight, tile, tile,
            lambda i: mod(i, C), lambda j: mod(j, C), lambda i: div(i, C), lambda j: div(j, C),
        )

    def column(ref):
        return jnp.sum(jnp.where(iota((C, C), 0) == iota((C, C), 1), ref[...], 0.0), 1, keepdims=True)

    bias = column(bias_ref)
    bias = (bias - jnp.mean(bias, axis=0, keepdims=True))[None]
    gain = column(gain_ref)[None]
    shift = column(shift_ref)[None]
    for first in range(0, rows, tile):
        for x in range(0, G, 2):
            hidden = jnp.concatenate(
                [fields_ref[x + k, first:first + tile] for k in range(2)], axis=-1
            )
            pre = dot(wbd_ref[...], hidden) + dot(
                rows_ref[first:first + tile, x * 2 * MZ:(x + 2) * 2 * MZ], depth_ref[...]
            )
            pre = pre.reshape(tile // C, C, 2 * Z) + bias
            spread = jnp.mean(pre * pre, axis=1, keepdims=True)
            normed = pre * (lax.rsqrt(spread + norm_eps) * gain) + shift
            value = (0.5 * normed) * (1.0 + lax.erf(normed * (0.5 ** 0.5)))
            value = value.astype(BF).reshape(tile, 2 * Z)
            for k in range(2):
                out_ref[x + k, first:first + tile] = value[:, k * Z:(k + 1) * Z]


def build(mesh):
    n_gx, n_gy, n_col = (mesh.shape[a] for a in ("gx", "gy", "col"))

    def local(fields, spectral, skip_weight, skip_bias, norm_gain, norm_shift):
        hidden = fields[0]
        xl, yl, C, Z = hidden.shape
        weights = spectral[0]
        kxl, kyl, _, _, dl, MZ = weights.shape
        X, Y, MX, MY = xl * n_gx, yl * n_gy, kxl * n_gx, kyl * n_gy
        G = min(8, xl)
        steps = xl // G
        L = 2 * kxl * MZ
        N, nxy = n_gx * n_gy * n_col, n_gx * n_gy

        cz, sz = cos_sin(np.arange(Z), np.arange(MZ), Z)
        forward = np.concatenate([cz, -sz], axis=1)
        depth_forward = np.kron(np.eye(G), forward)
        backward = np.concatenate([cz.T, -sz.T], axis=0) / math.sqrt(MX * MY * MZ)
        depth_backward = np.kron(np.eye(2), backward)
        cy, sy = cos_sin(np.arange(Y), signed(MY), Y)
        tyf = np.stack([cy, sy]).reshape(2, n_gy, yl, MY).transpose(1, 0, 3, 2)
        tyf = tyf.reshape(n_gy, 2 * MY, yl)
        tyi = np.stack([cy, sy]).reshape(2, n_gy, yl, MY).transpose(1, 2, 0, 3)
        tyi = tyi.reshape(n_gy, yl, 2 * MY)
        cx, sx = cos_sin(np.arange(X), signed(MX), X)
        f = np.stack([
            np.stack([np.stack([cx, -sx], 1), np.stack([sx, cx], 1)], 1),
            np.stack([np.stack([-sx, -cx], 1), np.stack([cx, -sx], 1)], 1),
        ]) / math.sqrt(X * Y * Z)
        f = f.reshape(2, n_gx, steps, G, 2, 2, n_gx, kxl).transpose(1, 2, 0, 3, 4, 6, 5, 7)
        txf = f.reshape(n_gx, steps, 2, 2 * G, 2 * MX)
        b = np.stack([
            np.stack([np.stack([cx, sx]), np.stack([-sx, cx])]),
            np.stack([np.stack([-sx, cx]), np.stack([-cx, -sx])]),
        ])
        b = b.reshape(2, 2, 2, n_gx, xl, n_gx, kxl).transpose(3, 0, 5, 1, 6, 4, 2)
        txi = b.reshape(n_gx, 2, 2 * MX, 2 * xl)
        const = lambda a: jnp.asarray(a.astype(np.float32)).astype(BF)

        cells = hidden.reshape(xl, yl * C, Z)
        halves = 2 if C % 32 == 0 and n_col % 2 == 0 else 1
        CH = C // halves
        turned = jnp.transpose(weights, (0, 1, 2, 4, 5, 3))

        def whole(shape):
            return pl.BlockSpec(shape, lambda *_: (0,) * len(shape))

        sizes = (n_gx, n_gy, n_col, xl, yl, C, MY, MZ, kxl, kyl, dl, G, steps, halves)
        tables = [const(t) for t in (depth_forward, tyf, txf, txi, tyi)]
        rows_both = pl.pallas_call(
            functools.partial(front_kernel, sizes),
            grid=(halves, steps),
            out_shape=jax.ShapeDtypeStruct((yl, C, xl * 2 * MZ), BF),
            in_specs=[
                pl.BlockSpec((G, yl, CH, Z), lambda h, i: (i, 0, h, 0)),
                pl.BlockSpec(memory_space=pl.ANY),
            ] + [whole(t.shape) for t in tables],
            out_specs=whole((yl, C, xl * 2 * MZ)),
            scratch_shapes=[
                pltpu.VMEM((2 * MY * CH, yl * CH), BF),
                pltpu.VMEM((steps, 2, G * 2 * MZ, 2 * MX * MZ), BF),
                pltpu.VMEM((MY * CH, 2 * MX * MZ), F32),
                pltpu.VMEM((halves, n_gx, n_gy, kyl * CH, L), BF),
                pltpu.VMEM((halves, nxy, kyl * CH, L), BF),
                pltpu.VMEM((n_col, halves, kyl * CH, L), BF),
                pltpu.VMEM((n_col, kyl * dl, L), BF),
                pltpu.VMEM((n_gx, n_gy, n_col, kyl * dl, L), BF),
                pltpu.VMEM((2, 2 * MX * MZ, 2 * xl * MZ), BF),
                pltpu.VMEM((yl * CH, 2 * MY * CH), BF),
                pltpu.VMEM((MY * C, MY * C), BF),
                pltpu.VMEM(turned.shape, BF),
                pltpu.VMEM((kyl, dl, C, L), F32),
                pltpu.VMEM((kyl, dl, C, L), F32),
                pltpu.SemaphoreType.DMA,
                pltpu.SemaphoreType.DMA((halves, nxy)),
                pltpu.SemaphoreType.DMA((halves, nxy)),
                pltpu.SemaphoreType.DMA((halves, n_col)),
                pltpu.SemaphoreType.DMA((halves, n_col)),
                pltpu.SemaphoreType.DMA((N,)),
                pltpu.SemaphoreType.DMA((N,)),
            ],
            compiler_params=pltpu.CompilerParams(
                collective_id=0, has_side_effects=True, vmem_limit_bytes=34 * 2**20,
                dimension_semantics=("arbitrary", "arbitrary"),
            ),
            name="front",
        )(hidden, turned, *tables).reshape(yl * C, xl * 2 * MZ)

        G2 = min(4, xl)
        rows = yl * C
        tile = min(256, rows)
        out = pl.pallas_call(
            functools.partial(back_kernel, (G2, C, MZ, Z, rows, tile)),
            grid=(xl // G2,),
            out_shape=jax.ShapeDtypeStruct(cells.shape, BF),
            in_specs=[
                pl.BlockSpec((rows, G2 * 2 * MZ), lambda i: (0, i)),
                pl.BlockSpec((G2, rows, Z), lambda i: (i, 0, 0)),
                whole((4 * MZ, 2 * Z)), whole((C, C)), whole((1, C)), whole((1, C)), whole((1, C)),
            ],
            out_specs=pl.BlockSpec((G2, rows, Z), lambda i: (i, 0, 0)),
            scratch_shapes=[pltpu.VMEM((tile, tile), BF)],
            compiler_params=pltpu.CompilerParams(
                vmem_limit_bytes=20 * 2**20, dimension_semantics=("arbitrary",)
            ),
            name="back",
        )(
            rows_both, cells, const(depth_backward), skip_weight[0],
            skip_bias, norm_gain, norm_shift,
        )
        return out.reshape(1, xl, yl, C, Z)

    return local


def solution(mesh):
    placed = (
        P("col", "gx", "gy", None, None),
        P(None, "gx", "gy", None, None, "col", None),
        P(), P(), P(), P(),
    )
    return jax.shard_map(
        build(mesh), mesh=mesh, in_specs=placed,
        out_specs=P("col", "gx", "gy", None, None), check_vma=False,
    )
```

time: 75.3 us -> 65.3 us (0.87)
  Pallas kernels: 62.1 us -> 55.5 us
  local copies, waits for them, and re-layouts: 12.9 us -> 9.32 us
    pallas_call x1, Pallas kernels: 50.9 us -> 44.2 us  [local(): pl.pallas_call(functools.partial(front_kernel, sizes), grid=(halves, step...]
    another operation x3 -> x0, local copies, waits for them, and re-layouts: 2.21 us -> none  [the longest x1 0.74 us: local(): skip_bias[0][:, None]]
    unnamed x9 -> x24, local copies, waits for them, and re-layouts: 10.7 us -> 9.32 us
where the time goes in v2:
time: 65.3 us; the launch traced here: 64.9 us
  Pallas kernels  55.5 us (85%)
  local copies, waits for them, and re-layouts  9.32 us (14%)
    pallas_call x1, Pallas kernels, local(): pl.pallas_call(functools.partial(front_kernel, sizes), grid=(halves, step...  44.2 us
    pallas_call x1, Pallas kernels, local(): pl.pallas_call(functools.partial(back_kernel, (G2, C, MZ, Z, rows, tile))...  11.3 us
    unnamed x24, local copies, waits for them, and re-layouts  9.32 us

profile of v2, /device:TPU:31, one launch (start us, length us, event | category | flops | bytes accessed | tf_op | source)
XLA Modules:
  0.0 64.9 jit_solution(15654373122245593975)
XLA Ops:
  0.0 0.0 copy-start.11
  0.0 0.0 copy-start.10
  0.0 0.0 copy-start.9
  0.0 0.0 copy-start
  0.0 3.4 %copy-done = bf16[1,32,32,32,128]{4,3,2,1,0:T(8,128)(2,1)S(1)} copy-done((bf16[1,32,32,32,128]{4,3,2,1,0:T(8,128)(2,1)S(1)}, bf16[1,32,32,32,128]{4,3,2,1,0:T(8,128)(2,1)}, u32[]{:S(2)}) %copy-start) | copy-done | bytes 8388632
  3.4 0.0 copy-start.1
  3.4 1.6 %copy-done.1 = bf16[1,4,4,2,32,16,16]{4,6,5,3,2,1,0:T(8,128)(2,1)S(1)} copy-done((bf16[1,4,4,2,32,16,16]{4,6,5,3,2,1,0:T(8,128)(2,1)S(1)}, bf16[1,4,4,2,32,16,16]{4,6,5,3,2,1,0:T(8,128)(2,1)}, u32[]{:S(2)}) %copy-start.1) | copy-done | bytes 524312
  5.0 0.0 copy-start.2
  5.0 1.0 %copy-done.2 = bf16[1024,256]{1,0:T(8,128)(2,1)S(1)} copy-done((bf16[1024,256]{1,0:T(8,128)(2,1)S(1)}, bf16[1024,256]{1,0:T(8,128)(2,1)}, u32[]{:S(2)}) %copy-start.2) | copy-done | bytes 524312
  6.1 0.0 copy-start.3
  6.1 0.9 %copy-done.3 = bf16[4,4,2,16,32]{4,3,2,1,0:T(8,128)(2,1)S(1)} copy-done((bf16[4,4,2,16,32]{4,3,2,1,0:T(8,128)(2,1)S(1)}, bf16[4,4,2,16,32]{4,3,2,1,0:T(8,128)(2,1)}, u32[]{:S(2)}) %copy-start.3) | copy-done | bytes 32792
  7.0 0.0 copy-start.4
  7.0 0.8 %copy-done.4 = bf16[4,2,32,64]{3,2,1,0:T(8,128)(2,1)S(1)} copy-done((bf16[4,2,32,64]{3,2,1,0:T(8,128)(2,1)S(1)}, bf16[4,2,32,64]{3,2,1,0:T(8,128)(2,1)}, u32[]{:S(2)}) %copy-start.4) | copy-done | bytes 32792
  7.8 0.0 copy-start.5
  7.8 0.8 %copy-done.5 = bf16[4,32,32]{2,1,0:T(8,128)(2,1)S(1)} copy-done((bf16[4,32,32]{2,1,0:T(8,128)(2,1)S(1)}, bf16[4,32,32]{2,1,0:T(8,128)(2,1)}, u32[]{:S(2)}) %copy-start.5) | copy-done | bytes 8216
  8.6 0.0 copy-start.7
  8.6 0.8 %copy-done.7 = bf16[4,32,32]{2,1,0:T(8,128)(2,1)S(1)} copy-done((bf16[4,32,32]{2,1,0:T(8,128)(2,1)S(1)}, bf16[4,32,32]{2,1,0:T(8,128)(2,1)}, u32[]{:S(2)}) %copy-start.7) | copy-done | bytes 8216
  9.3 0.0 copy-start.6
  9.3 0.0 copy-start.8
  9.3 44.2 %front.1 = bf16[32,32,1024]{2,1,0:T(8,128)(2,1)S(1)} custom-call(bf16[32,32,32,128]{3,2,1,0:T(8,128)(2,1)S(1)} %bitcast.8, bf16[4,4,2,16,16,32]{5,4,3,2,1,0:T(8,128)(2,1)S(1)} %bitcast.11, bf16[1024,256]{1,0:T(8,128)(2,1)S(1)} %copy-done.2, bf16[4,32,32]{2,1,0:T(8,128)(2,1)S(1)} %copy-done.7, bf16[4,4,2,16,32]{4,3,2,1,0:T(8,128)(2,1)S(1)} %copy-done.3, ...), custom_call_target="tpu_custom_call" | custom-call | tf_op jit(solution)/shard_map/front/pallas_call | solution.py:351
  53.6 0.0 copy-done.11
  53.6 0.0 copy-done.10
  53.6 0.0 copy-done.9
  53.6 0.0 copy-done.6
  53.6 0.0 copy-done.8
  53.6 11.3 %back.1 = bf16[32,1024,128]{2,1,0:T(8,128)(2,1)} custom-call(bf16[1024,1024]{1,0:T(8,128)(2,1)S(1)} %bitcast.10, bf16[32,1024,128]{2,1,0:T(8,128)(2,1)S(1)} %bitcast.9, bf16[64,256]{1,0:T(8,128)(2,1)S(1)} %copy-done.6, bf16[32,32]{1,0:T(8,128)(2,1)S(1)} %bitcast.12, f32[1,32]{1,0:T(1,128)S(1)} %copy-done.9, f32[1,32]{1,0:T(1,128)S(1)} %copy-done.10, ...), custom_call_target="tpu_custom_call" | custom-call | tf_op jit(solution)/shard_map/back/pallas_call | solution.py:393
Async XLA Ops:
  0.0 53.6 %copy-start.11 = (f32[1,32]{1,0:T(1,128)S(1)}, f32[1,32]{1,0:T(1,128)}, u32[]{:S(2)}) copy-start(f32[1,32]{1,0:T(1,128)} %shift_ref.1) | copy-start | bytes 388
  0.0 53.6 %copy-start.10 = (f32[1,32]{1,0:T(1,128)S(1)}, f32[1,32]{1,0:T(1,128)}, u32[]{:S(2)}) copy-start(f32[1,32]{1,0:T(1,128)} %gain_ref.1) | copy-start | bytes 388
  0.0 53.6 %copy-start.9 = (f32[1,32]{1,0:T(1,128)S(1)}, f32[1,32]{1,0:T(1,128)}, u32[]{:S(2)}) copy-start(f32[1,32]{1,0:T(1,128)} %bias_ref.1) | copy-start | bytes 388
  0.0 3.4 %copy-start = (bf16[1,32,32,32,128]{4,3,2,1,0:T(8,128)(2,1)S(1)}, bf16[1,32,32,32,128]{4,3,2,1,0:T(8,128)(2,1)}, u32[]{:S(2)}) copy-start(bf16[1,32,32,32,128]{4,3,2,1,0:T(8,128)(2,1)} %param.12) | copy-start | bytes 25165828
  3.4 1.6 %copy-start.1 = (bf16[1,4,4,2,32,16,16]{4,6,5,3,2,1,0:T(8,128)(2,1)S(1)}, bf16[1,4,4,2,32,16,16]{4,6,5,3,2,1,0:T(8,128)(2,1)}, u32[]{:S(2)}) copy-start(bf16[1,4,4,2,32,16,16]{4,6,5,3,2,1,0:T(8,128)(2,1)} %param.13) | copy-start | bytes 1572868
  5.0 1.0 %copy-start.2 = (bf16[1024,256]{1,0:T(8,128)(2,1)S(1)}, bf16[1024,256]{1,0:T(8,128)(2,1)}, u32[]{:S(2)}) copy-start(bf16[1024,256]{1,0:T(8,128)(2,1)} %constant.19.depth_ref) | copy-start | bytes 1572868
  6.1 0.9 %copy-start.3 = (bf16[4,4,2,16,32]{4,3,2,1,0:T(8,128)(2,1)S(1)}, bf16[4,4,2,16,32]{4,3,2,1,0:T(8,128)(2,1)}, u32[]{:S(2)}) copy-start(bf16[4,4,2,16,32]{4,3,2,1,0:T(8,128)(2,1)} %constant.21.txf_ref) | copy-start | bytes 98308
  7.0 0.8 %copy-start.4 = (bf16[4,2,32,64]{3,2,1,0:T(8,128)(2,1)S(1)}, bf16[4,2,32,64]{3,2,1,0:T(8,128)(2,1)}, u32[]{:S(2)}) copy-start(bf16[4,2,32,64]{3,2,1,0:T(8,128)(2,1)} %constant.22.txi_ref) | copy-start | bytes 98308
  7.8 0.8 %copy-start.5 = (bf16[4,32,32]{2,1,0:T(8,128)(2,1)S(1)}, bf16[4,32,32]{2,1,0:T(8,128)(2,1)}, u32[]{:S(2)}) copy-start(bf16[4,32,32]{2,1,0:T(8,128)(2,1)} %constant.23.tyi_ref) | copy-start | bytes 24580
  8.6 0.8 %copy-start.7 = (bf16[4,32,32]{2,1,0:T(8,128)(2,1)S(1)}, bf16[4,32,32]{2,1,0:T(8,128)(2,1)}, u32[]{:S(2)}) copy-start(bf16[4,32,32]{2,1,0:T(8,128)(2,1)} %constant.20.tyf_ref) | copy-start | bytes 24580
  9.3 44.3 %copy-start.6 = (bf16[64,256]{1,0:T(8,128)(2,1)S(1)}, bf16[64,256]{1,0:T(8,128)(2,1)}, u32[]{:S(2)}) copy-start(bf16[64,256]{1,0:T(8,128)(2,1)} %constant.24.depth_ref) | copy-start | bytes 98308
  9.3 44.3 %copy-start.8 = (bf16[1,32,32]{2,1,0:T(8,128)(2,1)S(1)}, bf16[1,32,32]{2,1,0:T(8,128)(2,1)}, u32[]{:S(2)}) copy-start(bf16[1,32,32]{2,1,0:T(8,128)(2,1)} %param.14) | copy-start | bytes 6148

commit v3 on v2

--- a/solution.py
+++ b/solution.py
@@ -85,13 +85,24 @@
     per = n_col // halves
     half, step = pl.program_id(0), pl.program_id(1)
     gx, gy, col = lax.axis_index("gx"), lax.axis_index("gy"), lax.axis_index("col")
-    place = gx * n_gy + gy
-    me = place * n_col + col
-
-    def target(linear):
-        return (linear // (n_gy * n_col), (linear // n_col) % n_gy, linear % n_col)
+
+    unrolled = N <= 64
+    at_gx = [lax.rem(gx + a, n_gx) for a in range(n_gx)] if unrolled else None
+    at_gy = [lax.rem(gy + a, n_gy) for a in range(n_gy)] if unrolled else None
+    at_col = [lax.rem(col + a, n_col) for a in range(n_col)] if unrolled else None
+
+    def target(i):
+        a, b, c = i // (n_gy * n_col), (i // n_col) % n_gy, i % n_col
+        if unrolled:
+            return at_gx[a], at_gy[b], at_col[c]
+        return (gx + a) % n_gx, (gy + b) % n_gy, (col + c) % n_col
 
     def loop(low, high, body):
+        if unrolled:
+            for i in range(low, high):
+                body(i)
+            return
+
         def go(i, carry):
             body(i)
             return carry
@@ -104,7 +115,7 @@
         barrier = pltpu.get_barrier_semaphore()
 
         def greet(i):
-            px, py, pc = target((me + i) % N)
+            px, py, pc = target(i)
             pl.semaphore_signal(
                 barrier, inc=1, device_id={"gx": px, "gy": py, "col": pc}, device_id_type=MESH
             )
@@ -141,11 +152,11 @@
         total_ref[...] += term
 
     def scatter(h, i):
-        other = (place + i) % nxy
+        px, py, _ = target(i * n_col)
         return pltpu.make_async_remote_copy(
-            src_ref=send_ref.at[h, other // n_gy, other % n_gy], dst_ref=recv_ref.at[h, i],
+            src_ref=send_ref.at[h, px, py], dst_ref=recv_ref.at[h, i],
             send_sem=send1.at[h, i], recv_sem=recv1.at[h, i],
-            device_id={"gx": other // n_gy, "gy": other % n_gy}, device_id_type=MESH,
+            device_id={"gx": px, "gy": py}, device_id_type=MESH,
         )
 
     @pl.when(step == steps - 1)
@@ -235,7 +246,7 @@
         modes_ref[gx, gy, col] = mix_ref[col]
 
         def gather(i):
-            px, py, pc = target((me + i) % N)
+            px, py, pc = target(i)
             return pltpu.make_async_remote_copy(
                 src_ref=mix_ref.at[pc], dst_ref=modes_ref.at[gx, gy, col],
                 send_sem=send3.at[i], recv_sem=recv3.at[i],
@@ -381,7 +392,7 @@
                 pltpu.SemaphoreType.DMA((N,)),
             ],
             compiler_params=pltpu.CompilerParams(
-                collective_id=0, has_side_effects=True, vmem_limit_bytes=34 * 2**20,
+                collective_id=0, has_side_effects=True, vmem_limit_bytes=60 * 2**20,
                 dimension_semantics=("arbitrary", "arbitrary"),
             ),
             name="front",
@@ -402,7 +413,7 @@
             out_specs=pl.BlockSpec((G2, rows, Z), lambda i: (i, 0, 0)),
             scratch_shapes=[pltpu.VMEM((tile, tile), BF)],
             compiler_params=pltpu.CompilerParams(
-                vmem_limit_bytes=20 * 2**20, dimension_semantics=("arbitrary",)
+                vmem_limit_bytes=60 * 2**20, dimension_semantics=("arbitrary",)
             ),
             name="back",
         )(

time: 65.3 us -> 60 us (0.919)
  local copies, waits for them, and re-layouts: 9.32 us -> 0 us
  Pallas kernels: 55.5 us -> 59.4 us
    unnamed x24 -> x0, local copies, waits for them, and re-layouts: 9.32 us -> none
    pallas_call x1, Pallas kernels: 11.3 us -> 13.8 us  [local(): pl.pallas_call(functools.partial(back_kernel, (G2, C, MZ, Z, rows, tile))...]
    pallas_call x1, Pallas kernels: 44.2 us -> 45.6 us  [local(): pl.pallas_call(functools.partial(front_kernel, sizes), grid=(halves, step...]
where the time goes in v3:
time: 60 us; the launch traced here: 59.4 us
  Pallas kernels  59.4 us (99%)
    pallas_call x1, Pallas kernels, local(): pl.pallas_call(functools.partial(front_kernel, sizes), grid=(halves, step...  45.6 us
    pallas_call x1, Pallas kernels, local(): pl.pallas_call(functools.partial(back_kernel, (G2, C, MZ, Z, rows, tile))...  13.8 us

profile of v3, /device:TPU:31, one launch (start us, length us, event | category | flops | bytes accessed | tf_op | source)
XLA Modules:
  0.0 59.4 jit_solution(4539498544990857937)
XLA Ops:
  0.0 45.6 %front.1 = bf16[32,32,1024]{2,1,0:T(8,128)(2,1)} custom-call(bf16[32,32,32,128]{3,2,1,0:T(8,128)(2,1)} %bitcast.8, bf16[4,4,2,16,16,32]{5,4,3,2,1,0:T(8,128)(2,1)} %bitcast.11, bf16[1024,256]{1,0:T(8,128)(2,1)} %constant.19.depth_ref, bf16[4,32,32]{2,1,0:T(8,128)(2,1)} %constant.20.tyf_ref, bf16[4,4,2,16,32]{4,3,2,1,0:T(8,128)(2,1)} %constant.21.txf_ref, ...), custom_call_target="tpu_custom_call" | custom-call | tf_op jit(solution)/shard_map/front/pallas_call | solution.py:362
  45.6 13.8 %back.1 = bf16[32,1024,128]{2,1,0:T(8,128)(2,1)} custom-call(bf16[1024,1024]{1,0:T(8,128)(2,1)} %bitcast.10, bf16[32,1024,128]{2,1,0:T(8,128)(2,1)} %bitcast.9, bf16[64,256]{1,0:T(8,128)(2,1)} %constant.24.depth_ref, bf16[32,32]{1,0:T(8,128)(2,1)} %bitcast.12, f32[1,32]{1,0:T(1,128)} %bias_ref.1, f32[1,32]{1,0:T(1,128)} %gain_ref.1, f32[1,32]{1,0:T(1,128)} %shift_ref.1), custom_call_target="tpu_custom_call" | custom-call | tf_op jit(solution)/shard_map/back/pallas_call | solution.py:404

commit v4 on v3

--- a/solution.py
+++ b/solution.py
@@ -74,8 +74,8 @@
     sizes,
     fields_ref, spectral_ref, depth_ref, tyf_ref, txf_ref, txi_ref, tyi_ref,
     out_ref,
-    ky_ref, kx_ref, total_ref, send_ref, recv_ref, spec_ref, mix_ref, modes_ref, gx_ref, hy_ref,
-    cm_ref, w_ref, wa_ref, wb_ref,
+    ky_ref, kx_ref, total_ref, send_ref, recv_ref, mix_ref, modes_ref, gx_ref, hy_ref,
+    cm_ref, w_ref, wa_ref,
     wsem, send1, recv1, send2, recv2, send3, recv3,
 ):
     n_gx, n_gy, n_col, xl, yl, C, MY, MZ, kxl, kyl, dl, G, steps, halves = sizes
@@ -120,7 +120,8 @@
                 barrier, inc=1, device_id={"gx": px, "gy": py, "col": pc}, device_id_type=MESH
             )
 
-        loop(1, N, greet)
+        loop(1, nxy, lambda i: greet(i * n_col))
+        loop(1, n_col, greet)
         weights_copy.start()
 
         def put(first, value):
@@ -159,6 +160,28 @@
             device_id={"gx": px, "gy": py}, device_id_type=MESH,
         )
 
+    def share(i):
+        return pltpu.make_async_remote_copy(
+            src_ref=wa_ref.at[col], dst_ref=wa_ref.at[col],
+            send_sem=send2.at[i], recv_sem=recv2.at[i],
+            device_id={"col": target(i)[2]}, device_id_type=MESH,
+        )
+
+    @pl.when((half == 0) & (step == min(1, steps - 1)))
+    def _():
+        weights_copy.wait()
+        eye = (iota((C, C), 0) == iota((C, C), 1)).astype(F32).astype(BF)
+        for k in range(kyl):
+            for d in range(dl):
+                parts = [w_ref[j, k, r, d] for r in range(2) for j in range(kxl)]
+                wa_ref[col, k, d] = lax.dot_general(
+                    eye, jnp.concatenate(parts, axis=0), (((1,), (1,)), ((), ())),
+                    preferred_element_type=F32,
+                ).astype(BF)
+        pl.semaphore_wait(pltpu.get_barrier_semaphore(), nxy + n_col - 2)
+        for i in range(1, n_col):
+            share(i).start()
+
     @pl.when(step == steps - 1)
     def _():
         rows = kyl * CH
@@ -167,24 +190,10 @@
             for q in range(n_gy):
                 send_ref[half, b, q] = block[q * rows:(q + 1) * rows]
 
-        @pl.when(half == 0)
-        def _():
-            pl.semaphore_wait(pltpu.get_barrier_semaphore(), N - 1)
-
         loop(1, nxy, lambda i: scatter(half, i).start())
 
     @pl.when((half == halves - 1) & (step == steps - 1))
     def _():
-        weights_copy.wait()
-        eye = (iota((C, C), 0) == iota((C, C), 1)).astype(F32).astype(BF)
-        turn = lambda a: lax.dot_general(
-            eye, a, (((1,), (1,)), ((), ())), preferred_element_type=F32
-        )
-        for k in range(kyl):
-            for d in range(dl):
-                parts = [[w_ref[j, k, r, d] for j in range(kxl)] for r in range(2)]
-                wa_ref[k, d] = turn(jnp.concatenate(parts[0] + parts[1], axis=0))
-                wb_ref[k, d] = turn(jnp.concatenate(parts[1] + parts[0], axis=0))
         for cs in range(2):
             def put(first, value, cs=cs):
                 gx_ref[cs, pl.ds(first, value.shape[0]), :] = value
@@ -210,55 +219,50 @@
             (source == j).astype(F32) - jnp.where(same, 1.0 / C, 0.0)
         ).astype(BF)
 
-        def share(h, i):
-            return pltpu.make_async_remote_copy(
-                src_ref=spec_ref.at[col, h], dst_ref=spec_ref.at[col, h],
-                send_sem=send2.at[h, i], recv_sem=recv2.at[h, i],
-                device_id={"col": (col + i) % n_col}, device_id_type=MESH,
-            )
-
+        sums = {}
         for h in range(halves):
             total = send_ref[h, gx, gy].astype(F32)
             for i in range(1, nxy):
                 scatter(h, i).wait_recv()
                 total = total + recv_ref[h, i].astype(F32)
-            spec_ref[col, h] = total.astype(BF)
-            for i in range(1, n_col):
-                share(h, i).start()
-        for h in range(halves):
-            for i in range(1, n_col):
-                share(h, i).wait_recv()
-        for s in range(n_col):
-            left, right = [], []
-            for h in range(halves):
-                spec = spec_ref[s, h].astype(F32)
-                re, im = spec[:, :L // 2], spec[:, L // 2:]
-                left.append(jnp.concatenate([re, re], axis=-1))
-                right.append(jnp.concatenate([-im, im], axis=-1))
+            spec = total.astype(BF).astype(F32)
+            if h == 0:
+                for i in range(1, n_col):
+                    share(i).wait_recv()
+            re, im = spec[:, :L // 2], spec[:, L // 2:]
+            re = jnp.concatenate([re, re], axis=-1)
+            im = jnp.concatenate([im, im], axis=-1)
+            for q in range(n_col):
+                for k in range(kyl):
+                    rows, chans = slice(k * CH, (k + 1) * CH), slice(h * CH, (h + 1) * CH)
+                    weight = wa_ref[q, k, :, chans].astype(F32)
+                    new = [jnp.sum(v[rows][None] * weight, axis=1) for v in (re, im)]
+                    old = sums.get((q, k))
+                    sums[q, k] = new if old is None else [a + b for a, b in zip(old, new)]
+        for q in range(n_col):
             for k in range(kyl):
-                mixed = None
-                for h in range(halves):
-                    rows, chans = slice(k * CH, (k + 1) * CH), slice(h * CH, (h + 1) * CH)
-                    term = left[h][rows][None] * wa_ref[k, :, chans]
-                    term = term + right[h][rows][None] * wb_ref[k, :, chans]
-                    mixed = term if mixed is None else mixed + term
-                mix_ref[s, k * dl:(k + 1) * dl] = jnp.sum(mixed, axis=1).astype(BF)
-        modes_ref[gx, gy, col] = mix_ref[col]
+                first, second = sums[q, k]
+                turned_second = jnp.concatenate(
+                    [-second[:, L // 2:], second[:, :L // 2]], axis=-1
+                )
+                row = (q * kyl + k) * dl
+                mix_ref[row:row + dl] = (first + turned_second).astype(BF)
+        modes_ref[gx, gy] = mix_ref[...]
 
         def gather(i):
-            px, py, pc = target(i)
+            px, py, _ = target(i * n_col)
             return pltpu.make_async_remote_copy(
-                src_ref=mix_ref.at[pc], dst_ref=modes_ref.at[gx, gy, col],
+                src_ref=mix_ref, dst_ref=modes_ref.at[gx, gy],
                 send_sem=send3.at[i], recv_sem=recv3.at[i],
-                device_id={"gx": px, "gy": py, "col": pc}, device_id_type=MESH,
-            )
-
-        loop(1, N, lambda i: gather(i).start())
+                device_id={"gx": px, "gy": py}, device_id_type=MESH,
+            )
+
+        loop(1, nxy, lambda i: gather(i).start())
         for h in range(halves):
             loop(1, nxy, lambda i: scatter(h, i).wait_send())
-            for i in range(1, n_col):
-                share(h, i).wait_send()
-        loop(1, N, lambda i: gather(i).wait_recv())
+        for i in range(1, n_col):
+            share(i).wait_send()
+        loop(1, nxy, lambda i: gather(i).wait_recv())
         full = jnp.concatenate(
             [modes_ref[b].reshape(MY * C, L) for b in range(n_gx)], axis=-1
         )
@@ -269,7 +273,7 @@
             out_ref[:, h * CH:(h + 1) * CH] = dot(hy_ref[...], part).astype(BF).reshape(
                 yl, CH, out_ref.shape[-1]
             )
-        loop(1, N, lambda i: gather(i).wait_send())
+        loop(1, nxy, lambda i: gather(i).wait_send())
 
 
 def back_kernel(
@@ -374,22 +378,20 @@
                 pltpu.VMEM((MY * CH, 2 * MX * MZ), F32),
                 pltpu.VMEM((halves, n_gx, n_gy, kyl * CH, L), BF),
                 pltpu.VMEM((halves, nxy, kyl * CH, L), BF),
-                pltpu.VMEM((n_col, halves, kyl * CH, L), BF),
-                pltpu.VMEM((n_col, kyl * dl, L), BF),
-                pltpu.VMEM((n_gx, n_gy, n_col, kyl * dl, L), BF),
+                pltpu.VMEM((kyl * C, L), BF),
+                pltpu.VMEM((n_gx, n_gy, kyl * C, L), BF),
                 pltpu.VMEM((2, 2 * MX * MZ, 2 * xl * MZ), BF),
                 pltpu.VMEM((yl * CH, 2 * MY * CH), BF),
                 pltpu.VMEM((MY * C, MY * C), BF),
                 pltpu.VMEM(turned.shape, BF),
-                pltpu.VMEM((kyl, dl, C, L), F32),
-                pltpu.VMEM((kyl, dl, C, L), F32),
+                pltpu.VMEM((n_col, kyl, dl, C, L), BF),
                 pltpu.SemaphoreType.DMA,
                 pltpu.SemaphoreType.DMA((halves, nxy)),
                 pltpu.SemaphoreType.DMA((halves, nxy)),
-                pltpu.SemaphoreType.DMA((halves, n_col)),
-                pltpu.SemaphoreType.DMA((halves, n_col)),
-                pltpu.SemaphoreType.DMA((N,)),
-                pltpu.SemaphoreType.DMA((N,)),
+                pltpu.SemaphoreType.DMA((n_col,)),
+                pltpu.SemaphoreType.DMA((n_col,)),
+                pltpu.SemaphoreType.DMA((nxy,)),
+                pltpu.SemaphoreType.DMA((nxy,)),
             ],
             compiler_params=pltpu.CompilerParams(
                 collective_id=0, has_side_effects=True, vmem_limit_bytes=60 * 2**20,

time: 60 us -> 58 us (0.967)
  Pallas kernels: 59.4 us -> 57.6 us
    pallas_call x1, Pallas kernels: 45.6 us -> 43.8 us  [local(): pl.pallas_call(functools.partial(front_kernel, sizes), grid=(halves, step...]
where the time goes in v4:
time: 58 us; the launch traced here: 57.6 us
  Pallas kernels  57.6 us (99%)
    pallas_call x1, Pallas kernels, local(): pl.pallas_call(functools.partial(front_kernel, sizes), grid=(halves, step...  43.8 us
    pallas_call x1, Pallas kernels, local(): pl.pallas_call(functools.partial(back_kernel, (G2, C, MZ, Z, rows, tile))...  13.8 us

profile of v4, /device:TPU:31, one launch (start us, length us, event | category | flops | bytes accessed | tf_op | source)
XLA Modules:
  0.0 57.6 jit_solution(13501803903032415468)
XLA Ops:
  0.0 43.8 %front.1 = bf16[32,32,1024]{2,1,0:T(8,128)(2,1)} custom-call(bf16[32,32,32,128]{3,2,1,0:T(8,128)(2,1)} %bitcast.8, bf16[4,4,2,16,16,32]{5,4,3,2,1,0:T(8,128)(2,1)} %bitcast.11, bf16[1024,256]{1,0:T(8,128)(2,1)} %constant.19.depth_ref, bf16[4,32,32]{2,1,0:T(8,128)(2,1)} %constant.20.tyf_ref, bf16[4,4,2,16,32]{4,3,2,1,0:T(8,128)(2,1)} %constant.21.txf_ref, ...), custom_call_target="tpu_custom_call" | custom-call | tf_op jit(solution)/shard_map/front/pallas_call | solution.py:366
  43.8 13.8 %back.1 = bf16[32,1024,128]{2,1,0:T(8,128)(2,1)} custom-call(bf16[1024,1024]{1,0:T(8,128)(2,1)} %bitcast.10, bf16[32,1024,128]{2,1,0:T(8,128)(2,1)} %bitcast.9, bf16[64,256]{1,0:T(8,128)(2,1)} %constant.24.depth_ref, bf16[32,32]{1,0:T(8,128)(2,1)} %bitcast.12, f32[1,32]{1,0:T(1,128)} %bias_ref.1, f32[1,32]{1,0:T(1,128)} %gain_ref.1, f32[1,32]{1,0:T(1,128)} %shift_ref.1), custom_call_target="tpu_custom_call" | custom-call | tf_op jit(solution)/shard_map/back/pallas_call | solution.py:406
